TPU v7x, 32 devices: a whole 2x2x4 slice. The times are simulated.
32 devices in a mesh: orb: 16 (over z, y, core), grid: 2 (over x).
Axes of the slice: x: 2, y: 2, z: 4, core: 2. Of those that a mesh axis runs over, the one named last changes fastest.
Arguments:
- orbitals: bfloat16 [32, 11520], P('orb', 'grid'), may hold values from -1.5 to 1.5
- occupation: bfloat16 [32], P('orb'), may hold values from 0.29882812 to 1
Outputs:
- potentials: float32 [32, 11520], P('orb', 'grid')
- projectors: float32 [32, 11520], P('orb', 'grid')
All inputs are finite; a program needn't handle non-finite values.
Results may differ from a plain program's by a relative error of at most 0.0025.
Values may be sent and summed in bfloat16 or wider, within the bound.
No kernel may reach another device: no remote copies, remote signals or barrier semaphores. Data moves between devices by JAX's collectives and lax.ppermute only.
A program may use at most 64 MiB of HBM per device.

v0:
```python
import math
import jax
import jax.numpy as jnp
from jax import lax
from jax.sharding import PartitionSpec as P

NX = 20
NY = 24
NZ = 24
NPTS = 11520


def hartley_table(length):
    index = jnp.arange(length, dtype=jnp.int32)
    product = index[:, None] * index[None, :] % length
    angle = 2.0 * math.pi / length * product.astype(jnp.float32)
    return (jnp.cos(angle) + jnp.sin(angle)).astype(jnp.bfloat16)


def signed_square(length):
    index = jnp.arange(length, dtype=jnp.int32)
    signed = jnp.where(index <= length // 2, index, index - length).astype(jnp.float32)
    return (2.0 * math.pi * signed / length) ** 2


def coulomb_kernel(size_x, size_y, size_z):
    total = (
        signed_square(size_x)[:, None, None]
        + signed_square(size_y)[None, :, None]
        + signed_square(size_z)[None, None, :]
    )
    safe = jnp.where(total > 0, total, 1.0)
    return jnp.where(total > 0, 1.0 / safe, 0.0) / (size_x * size_y * size_z)


def solve_pairs(density, table_x, table_y, table_z, kernel):
    section = jnp.einsum(
        "ax,pxyz->payz", table_x, density, preferred_element_type=jnp.float32
    ).astype(jnp.bfloat16)
    section = jnp.einsum(
        "by,pxyz->pxbz", table_y, section, preferred_element_type=jnp.float32
    ).astype(jnp.bfloat16)
    spectrum = jnp.einsum("cz,pxyz->pxyc", table_z, section, preferred_element_type=jnp.float32)
    section = (spectrum * kernel).astype(jnp.bfloat16)
    section = jnp.einsum(
        "cz,pxyz->pxyc", table_z, section, preferred_element_type=jnp.float32
    ).astype(jnp.bfloat16)
    section = jnp.einsum(
        "by,pxyz->pxbz", table_y, section, preferred_element_type=jnp.float32
    ).astype(jnp.bfloat16)
    return jnp.einsum("ax,pxyz->payz", table_x, section, preferred_element_type=jnp.float32)


def pair_folder(targets, running, pieces):
    table_x = hartley_table(NX)
    table_y = hartley_table(NY)
    table_z = hartley_table(NZ)
    kernel = coulomb_kernel(NX, NY, NZ)
    target_rows = targets.astype(jnp.float32)
    target_count = targets.shape[0]
    block, block_weight = pieces
    rows = block.shape[0]
    group = math.gcd(rows, 64)
    blocks = block.reshape(rows // group, group, NPTS)
    weights = block_weight.astype(jnp.float32).reshape(rows // group, group)

    def accumulate(totals, inputs):
        sources, source_weight = inputs
        source_rows = sources.astype(jnp.float32)
        density = (target_rows[:, None, :] * source_rows[None, :, :]).astype(jnp.bfloat16)
        density = density.reshape(target_count * group, NX, NY, NZ)
        potential = solve_pairs(density, table_x, table_y, table_z, kernel).reshape(
            target_count, group, NPTS
        )
        weighted = source_weight[None, :, None] * potential * source_rows[None, :, :]
        return (totals - jnp.sum(weighted, axis=1), None)

    result, unused = lax.scan(accumulate, running, (blocks, weights))
    return result


def on_device(orbitals, occupation):
    own_count = orbitals.shape[0]
    per_device = own_count // lax.axis_size("grid")
    empty = jnp.zeros((per_device, NPTS), jnp.float32)
    whole = lax.all_gather(orbitals, "grid", axis=1, tiled=True)
    targets = lax.dynamic_slice_in_dim(whole, lax.axis_index("grid") * per_device, per_device, 0)
    totals = pair_folder(
        targets,
        empty,
        (
            lax.all_gather(whole, "orb", axis=0, tiled=True),
            lax.all_gather(occupation, "orb", axis=0, tiled=True),
        ),
    )
    potentials = lax.all_to_all(totals, "grid", split_axis=1, concat_axis=0, tiled=True)
    source_points, potential_points = (
        lax.all_to_all(
            orbitals.astype(jnp.float32), "orb", split_axis=1, concat_axis=0, tiled=True
        ),
        lax.all_to_all(potentials, "orb", split_axis=1, concat_axis=0, tiled=True),
    )
    partial_gram = (
        lax.dot_general(
            source_points,
            potential_points,
            (((1,), (1,)), ((), ())),
            precision=lax.Precision.HIGHEST,
        )
        / NPTS
    )
    gram = lax.psum(partial_gram, ("orb", "grid"))
    factor = jnp.linalg.cholesky(-gram)
    identity = jnp.eye(gram.shape[0], dtype=jnp.float32)
    inverse = lax.linalg.triangular_solve(factor, identity, left_side=True, lower=True)
    projector_points = jnp.dot(inverse, potential_points, precision=lax.Precision.HIGHEST)
    projectors = lax.all_to_all(projector_points, "orb", split_axis=0, concat_axis=1, tiled=True)
    return (potentials, projectors)


def solution(mesh):
    placed = (P("orb", "grid"), P("orb"))
    return jax.shard_map(
        on_device,
        mesh=mesh,
        in_specs=placed,
        out_specs=(P("orb", "grid"), P("orb", "grid")),
        check_vma=False,
    )
```

profile of v0, /device:TPU:0, one launch (start us, length us, event | category | flops | bytes accessed | tf_op | source)
XLA Modules:
  0.0 226.1 jit_solution(919936937522886090)
XLA Ops:
  0.7 5.7 %all_gather.10 = bf16[2,11520]{1,0:T(2,128)(2,1)S(1)} all-gather(bf16[2,5760]{1,0:T(2,128)(2,1)} %param.2), channel_id=1, replica_groups=mesh['orb'=16,'grid'=2] {'grid'}, dimensions={1}, use_global_device_ids=true | all-gather | bytes 69120 | tf_op jit(solution)/shard_map/all_gather | solution.py:86
  6.3 24.3 %all-gather = bf16[16,2,11520]{2,1,0:T(2,128)(2,1)S(1)} all-gather(bf16[1,2,11520]{2,1,0:T(2,128)(2,1)S(1)} %bitcast.58), channel_id=1, replica_groups=mesh['orb'=16,'grid'=2] {'orb'}, dimensions={0}, use_global_device_ids=true | all-gather | bytes 783360 | tf_op jit(solution)/shard_map/all_gather | solution.py:92
  30.7 6.4 %reshape.167 = f32[32,20,24,24]{3,2,1,0:T(8,128)} reshape(bf16[16,2,11520]{2,1,0:T(2,128)(2,1)S(1)} %all-gather) | data formatting | bytes 2211840 | tf_op jit(solution)/shard_map/while/body/eval_jaxpr/convert_element_type | solution.py:69
  37.1 1.3 reshape.174
  38.8 3.9 %multiply_convert_fusion.1 = bf16[32,20,24,24]{3,2,1,0:T(8,128)(2,1)S(1)} fusion(f32[32,20,24,24]{3,2,1,0:T(8,128)} %reshape.167, f32[20,24,24]{2,1,0:T(8,128)S(1)} %reshape.166), kind=kLoop, calls=%fused_computation.1 | loop fusion | flops 737280 | bytes 2257920 | tf_op jit(solution)/shard_map/while/body/eval_jaxpr/convert_element_type | solution.py:70
  42.6 4.9 %convert_bitcast_fusion = bf16[32,20,24,24]{1,3,2,0:T(8,128)(2,1)} fusion(bf16[32,20,24,24]{3,2,1,0:T(8,128)(2,1)S(1)} %multiply_convert_fusion.1), kind=kOutput, calls=%fused_computation.4 | convolution fusion | flops 15118640 | bytes 1474560 | tf_op jit(solution)/shard_map/while/body/eval_jaxpr/ax,pxyz->payz/dot_general | solution.py:37
  47.5 8.5 %copy.24 = bf16[32,20,24,24]{2,3,1,0:T(8,128)(2,1)} copy(bf16[32,20,24,24]{1,3,2,0:T(8,128)(2,1)} %convert_bitcast_fusion) | data formatting | bytes 1474560 | tf_op jit(solution)/shard_map/while/body/eval_jaxpr/convert_element_type | solution.py:39
  56.0 5.2 %fusion.44 = bf16[32,20,24,24]{3,2,1,0:T(8,128)(2,1)} fusion(bf16[32,20,24,24]{2,3,1,0:T(8,128)(2,1)} %copy.24), kind=kOutput, calls=%fused_computation.53 | convolution fusion | flops 17701056 | bytes 1474560 | tf_op jit(solution)/shard_map/while/body/eval_jaxpr/by,pxyz->pxbz/dot_general | solution.py:40
  61.5 7.4 %fusion.2 = bf16[32,20,24,24]{3,2,1,0:T(8,128)(2,1)} fusion(f32[20,24,24]{2,1,0:T(8,128)S(1)} %fusion.19, bf16[32,20,24,24]{3,2,1,0:T(8,128)(2,1)} %fusion.44), kind=kOutput, calls=%fused_computation.5 | convolution fusion | flops 36139392 | bytes 1520640 | tf_op jit(solution)/shard_map/while/body/eval_jaxpr/cz,pxyz->pxyc/dot_general | solution.py:45
  68.9 5.4 %convert_bitcast_fusion.1 = bf16[32,20,24,24]{2,3,1,0:T(8,128)(2,1)} fusion(bf16[32,20,24,24]{3,2,1,0:T(8,128)(2,1)} %fusion.2), kind=kOutput, calls=%fused_computation.8 | convolution fusion | flops 18069696 | bytes 1474560 | tf_op jit(solution)/shard_map/while/body/eval_jaxpr/by,pxyz->pxbz/dot_general | solution.py:48
  74.3 10.1 %copy.27 = bf16[32,20,24,24]{0,1,3,2:T(8,128)(2,1)S(1)} copy(bf16[32,20,24,24]{2,3,1,0:T(8,128)(2,1)} %convert_bitcast_fusion.1) | data formatting | bytes 1474560 | tf_op jit(solution)/shard_map/while/body/eval_jaxpr/convert_element_type | solution.py:50
  84.4 4.0 %convolution_bitcast_fusion = f32[32,20,24,24]{0,1,3,2:T(8,128)} fusion(bf16[32,20,24,24]{0,1,3,2:T(8,128)(2,1)S(1)} %copy.27), kind=kOutput, calls=%fused_computation.13 | convolution fusion | flops 14750000 | bytes 2211840 | tf_op jit(solution)/shard_map/while/body/eval_jaxpr/ax,pxyz->payz/dot_general | solution.py:51
  88.4 12.1 %copy.28 = f32[32,20,24,24]{3,2,1,0:T(8,128)} copy(f32[32,20,24,24]{0,1,3,2:T(8,128)} %convolution_bitcast_fusion) | data formatting | bytes 2949120 | tf_op jit(solution)/shard_map/while/body/eval_jaxpr/ax,pxyz->payz/transpose | solution.py:51
  102.0 6.8 %reshape.165 = f32[32,11520]{1,0:T(8,128)S(1)} reshape(f32[32,20,24,24]{3,2,1,0:T(8,128)} %copy.28) | data formatting | bytes 2949120 | tf_op jit(solution)/shard_map/while/body/eval_jaxpr/reshape | solution.py:72
  108.9 29.9 %all-reduce = bf16[32]{0:T(256)(128)(2,1)S(1)} all-reduce(bf16[32]{0:T(256)(128)(2,1)S(1)} %dynamic-update-slice.3), channel_id=1, replica_groups=mesh['orb'=16,'grid'=2] {'orb'}, use_global_device_ids=true, to_apply=%add | all-reduce | flops 32 | bytes 128
  139.1 0.7 sub.25
  139.7 3.3 %all-to-all-start = ((f32[1,2,5760]{2,0,1:T(1,128)}), f32[1,2,5760]{2,0,1:T(1,128)S(1)}, u32[]{:S(2)}, u32[]{:S(2)}) async-start(f32[1,2,5760]{2,0,1:T(1,128)} %sub.25), calls=%async_computation | async-start | bytes 92160 | tf_op jit(solution)/shard_map/all_to_all | solution.py:96
  143.8 3.2 %all-to-all-done = f32[1,2,5760]{2,0,1:T(1,128)S(1)} async-done(((f32[1,2,5760]{2,0,1:T(1,128)}), f32[1,2,5760]{2,0,1:T(1,128)S(1)}, u32[]{:S(2)}, u32[]{:S(2)}) %all-to-all-start) | async-done | bytes 46112 | tf_op jit(solution)/shard_map/all_to_all | solution.py:96
  147.0 3.5 %all-to-all-start.2 = ((f32[2,16,360]{2,0,1:T(2,128)}), f32[2,16,360]{2,0,1:T(2,128)S(1)}, u32[]{:S(2)}, u32[]{:S(2)}) async-start(f32[2,16,360]{2,0,1:T(2,128)} %copy.30), calls=%async_computation.2 | async-start | bytes 98304 | tf_op jit(solution)/shard_map/all_to_all | solution.py:98
  150.8 0.6 copy.29
  151.4 5.8 %all-to-all-done.2 = f32[2,16,360]{2,0,1:T(2,128)S(1)} async-done(((f32[2,16,360]{2,0,1:T(2,128)}), f32[2,16,360]{2,0,1:T(2,128)S(1)}, u32[]{:S(2)}, u32[]{:S(2)}) %all-to-all-start.2) | async-done | bytes 46112 | tf_op jit(solution)/shard_map/all_to_all | solution.py:98
  157.3 3.5 %all-to-all-start.1 = ((f32[2,16,360]{2,0,1:T(2,128)}), f32[2,16,360]{2,0,1:T(2,128)S(1)}, u32[]{:S(2)}, u32[]{:S(2)}) async-start(f32[2,16,360]{2,0,1:T(2,128)} %copy.29), calls=%async_computation.1 | async-start | bytes 98304 | tf_op jit(solution)/shard_map/all_to_all | solution.py:101
  160.8 6.7 %all-to-all-done.1 = f32[2,16,360]{2,0,1:T(2,128)S(1)} async-done(((f32[2,16,360]{2,0,1:T(2,128)}), f32[2,16,360]{2,0,1:T(2,128)S(1)}, u32[]{:S(2)}, u32[]{:S(2)}) %all-to-all-start.1) | async-done | bytes 46112 | tf_op jit(solution)/shard_map/all_to_all | solution.py:101
  167.8 38.0 %psum.7 = f32[32,32]{0,1:T(8,128)S(1)} all-reduce(f32[32,32]{0,1:T(8,128)S(1)} %fusion.17), channel_id=1, replica_groups=mesh['orb'=16,'grid'=2] {'orb','grid'}, use_global_device_ids=true, to_apply=%region_1.2 | all-reduce | flops 1024 | bytes 8192 | tf_op jit(solution)/shard_map/psum | solution.py:112
  205.8 2.9 %cholesky.17 = f32[32,32]{1,0:T(8,128)S(1)} custom-call(f32[32,32]{1,0:T(8,128)S(1)} %fusion.22), custom_call_target="Cholesky" | custom-call | tf_op jit(solution)/shard_map/jit(cholesky)/cholesky | solution.py:113
  208.8 0.6 compare_reduce_fusion
  209.4 0.7 fusion.21
  210.1 2.4 %custom-call.6 = f32[1,32,32]{1,2,0:T(8,128)S(1)} custom-call(f32[1,32,32]{2,1,0:T(8,128)S(1)} %fusion.21), custom_call_target="InvertDiagBlocksLowerTriangular" | custom-call | tf_op jit(solution)/shard_map/triangular_solve | solution.py:115
  213.0 0.6 copy.34
  213.6 5.0 %all-to-all-start.3 = ((f32[16,2,360]{2,1,0:T(2,128)}), f32[16,2,360]{2,1,0:T(2,128)S(1)}, u32[]{:S(2)}, u32[]{:S(2)}) async-start(f32[16,2,360]{2,1,0:T(2,128)} %copy.34), calls=%async_computation.3 | async-start | bytes 98304 | tf_op jit(solution)/shard_map/all_to_all | solution.py:117
  219.3 6.1 %all-to-all-done.3 = f32[16,2,360]{2,1,0:T(2,128)S(1)} async-done(((f32[16,2,360]{2,1,0:T(2,128)}), f32[16,2,360]{2,1,0:T(2,128)S(1)}, u32[]{:S(2)}, u32[]{:S(2)}) %all-to-all-start.3) | async-done | bytes 46112 | tf_op jit(solution)/shard_map/all_to_all | solution.py:117
  225.4 0.8 all_to_all.65
  (37 shorter events, 4.2 us)
Async XLA Ops:
  88.4 12.1 %copy-start.3 = (u32[32]{0:T(128)S(1)}, u32[32]{0:T(128)}, u32[]{:S(2)}) copy-start(u32[32]{0:T(128)} %constant.125) | copy-start | bytes 388
  88.4 13.4 %copy-start.2 = (bf16[2]{0:T(256)(128)(2,1)S(1)}, bf16[2]{0:T(256)(128)(2,1)}, u32[]{:S(2)}) copy-start(bf16[2]{0:T(256)(128)(2,1)} %param.3) | copy-start | bytes 16
  102.0 36.7 %copy-start = (f32[32,11520]{1,0:T(8,128)S(1)}, f32[32,11520]{1,0:T(8,128)}, u32[]{:S(2)}) copy-start(f32[32,11520]{1,0:T(8,128)} %reshape.174) | copy-start | bytes 4423684
  102.0 41.0 %copy-start.1 = (bf16[2,5760]{1,0:T(2,128)(2,1)S(1)}, bf16[2,5760]{1,0:T(2,128)(2,1)}, u32[]{:S(2)}) copy-start(bf16[2,5760]{1,0:T(2,128)(2,1)} %param.2) | copy-start | bytes 69124
  139.7 7.3 %all-to-all-start = ((f32[1,2,5760]{2,0,1:T(1,128)}), f32[1,2,5760]{2,0,1:T(1,128)S(1)}, u32[]{:S(2)}, u32[]{:S(2)}) async-start(f32[1,2,5760]{2,0,1:T(1,128)} %sub.25), calls=%async_computation | async-start | bytes 92160 | tf_op jit(solution)/shard_map/all_to_all | solution.py:96
  147.0 10.2 %all-to-all-start.2 = ((f32[2,16,360]{2,0,1:T(2,128)}), f32[2,16,360]{2,0,1:T(2,128)S(1)}, u32[]{:S(2)}, u32[]{:S(2)}) async-start(f32[2,16,360]{2,0,1:T(2,128)} %copy.30), calls=%async_computation.2 | async-start | bytes 98304 | tf_op jit(solution)/shard_map/all_to_all | solution.py:98
  157.3 10.2 %all-to-all-start.1 = ((f32[2,16,360]{2,0,1:T(2,128)}), f32[2,16,360]{2,0,1:T(2,128)S(1)}, u32[]{:S(2)}, u32[]{:S(2)}) async-start(f32[2,16,360]{2,0,1:T(2,128)} %copy.29), calls=%async_computation.1 | async-start | bytes 98304 | tf_op jit(solution)/shard_map/all_to_all | solution.py:101
  213.6 11.8 %all-to-all-start.3 = ((f32[16,2,360]{2,1,0:T(2,128)}), f32[16,2,360]{2,1,0:T(2,128)S(1)}, u32[]{:S(2)}, u32[]{:S(2)}) async-start(f32[16,2,360]{2,1,0:T(2,128)} %copy.34), calls=%async_computation.3 | async-start | bytes 98304 | tf_op jit(solution)/shard_map/all_to_all | solution.py:117
where the time goes:
time: 227 us; the launch traced here: 226 us
  blocking collectives  97.9 us (43%)
  local copies, waits for them, and re-layouts  50.8 us (22%)
  matrix products  27.5 us (12%)
  waiting for transfers between devices  21.9 us (10%)
  starting transfers between devices  15.3 us (7%)
  other arithmetic  11.4 us (5%)
    psum x1, blocking collectives, on_device(): gram = lax.psum(partial_gram, ('orb', 'grid'))  38 us
    unnamed x1, blocking collectives  29.9 us
    all_gather x1, blocking collectives, on_device(): lax.all_gather(whole, 'orb', axis=0, tiled=True)  24.3 us
    transpose x1, local copies, waits for them, and re-layouts, solve_pairs(): jnp.einsum('ax,pxyz->payz', table_x, section, preferred_element_type=jnp....  12.1 us
    dot_general x2, matrix products, solve_pairs(): jnp.einsum('by,pxyz->pxbz', table_y, section, preferred_element_type=jnp....  10.6 us
    convert_element_type x1, local copies, waits for them, and re-layouts, solve_pairs(): section = jnp.einsum('by,pxyz->pxbz', table_y, section, preferred_element...  10.1 us
    convert_element_type x1, local copies, waits for them, and re-layouts, solve_pairs(): section = jnp.einsum('ax,pxyz->payz', table_x, density, preferred_element...  8.51 us
    convert_element_type x2, local copies, waits for them, and re-layouts, accumulate(): source_rows = sources.astype(jnp.float32)  7.76 us
  transfers between devices with their start and end apart: 4, of which 4 were waited for; matrix products, arithmetic and copies ran while one was open for 1% of the time, Pallas kernels for 0%

commit v1 on v0

--- a/solution.py
+++ b/solution.py
@@ -114,7 +114,12 @@
     identity = jnp.eye(gram.shape[0], dtype=jnp.float32)
     inverse = lax.linalg.triangular_solve(factor, identity, left_side=True, lower=True)
     projector_points = jnp.dot(inverse, potential_points, precision=lax.Precision.HIGHEST)
-    projectors = lax.all_to_all(projector_points, "orb", split_axis=0, concat_axis=1, tiled=True)
+    projectors = jnp.concatenate(
+        lax.all_to_all(
+            jnp.stack(jnp.split(projector_points, lax.axis_size("orb"), axis=0)), "orb", 0, 0
+        ),
+        axis=1,
+    )
     return (potentials, projectors)
 
 

time: 227 us -> 236 us (1.040)
  local copies, waits for them, and re-layouts: 50.8 us -> 59.5 us
    unnamed x12 -> x27, local copies, waits for them, and re-layouts: 1.49 us -> 10.3 us
where the time goes in v1:
time: 236 us; the launch traced here: 235 us
  blocking collectives  97.9 us (41%)
  local copies, waits for them, and re-layouts  59.5 us (25%)
  matrix products  27.6 us (12%)
  waiting for transfers between devices  21.9 us (9%)
  starting transfers between devices  15.3 us (6%)
  other arithmetic  11.4 us (5%)
    psum x1, blocking collectives, on_device(): gram = lax.psum(partial_gram, ('orb', 'grid'))  38 us
    unnamed x1, blocking collectives  29.9 us
    all_gather x1, blocking collectives, on_device(): lax.all_gather(whole, 'orb', axis=0, tiled=True)  24.3 us
    transpose x1, local copies, waits for them, and re-layouts, solve_pairs(): jnp.einsum('ax,pxyz->payz', table_x, section, preferred_element_type=jnp....  12.1 us
    dot_general x2, matrix products, solve_pairs(): jnp.einsum('by,pxyz->pxbz', table_y, section, preferred_element_type=jnp....  10.6 us
    unnamed x27, local copies, waits for them, and re-layouts  10.3 us
    convert_element_type x1, local copies, waits for them, and re-layouts, solve_pairs(): section = jnp.einsum('by,pxyz->pxbz', table_y, section, preferred_element...  10.1 us
    convert_element_type x1, local copies, waits for them, and re-layouts, solve_pairs(): section = jnp.einsum('ax,pxyz->payz', table_x, density, preferred_element...  8.51 us
  transfers between devices with their start and end apart: 4, of which 4 were waited for; matrix products, arithmetic and copies ran while one was open for 1% of the time, Pallas kernels for 0%

profile of v1, /device:TPU:0, one launch (start us, length us, event | category | flops | bytes accessed | tf_op | source)
XLA Modules:
  0.0 234.9 jit_solution(9939405017746769419)
XLA Ops:
  0.7 5.7 %all_gather.10 = bf16[2,11520]{1,0:T(2,128)(2,1)S(1)} all-gather(bf16[2,5760]{1,0:T(2,128)(2,1)} %param.2), channel_id=1, replica_groups=mesh['orb'=16,'grid'=2] {'grid'}, dimensions={1}, use_global_device_ids=true | all-gather | bytes 69120 | tf_op jit(solution)/shard_map/all_gather | solution.py:86
  6.3 24.3 %all-gather = bf16[16,2,11520]{2,1,0:T(2,128)(2,1)S(1)} all-gather(bf16[1,2,11520]{2,1,0:T(2,128)(2,1)S(1)} %bitcast.119), channel_id=1, replica_groups=mesh['orb'=16,'grid'=2] {'orb'}, dimensions={0}, use_global_device_ids=true | all-gather | bytes 783360 | tf_op jit(solution)/shard_map/all_gather | solution.py:92
  30.7 6.4 %reshape.169 = f32[32,20,24,24]{3,2,1,0:T(8,128)} reshape(bf16[16,2,11520]{2,1,0:T(2,128)(2,1)S(1)} %all-gather) | data formatting | bytes 2211840 | tf_op jit(solution)/shard_map/while/body/eval_jaxpr/convert_element_type | solution.py:69
  37.1 1.3 reshape.176
  38.8 3.9 %multiply_convert_fusion.1 = bf16[32,20,24,24]{3,2,1,0:T(8,128)(2,1)S(1)} fusion(f32[32,20,24,24]{3,2,1,0:T(8,128)} %reshape.169, f32[20,24,24]{2,1,0:T(8,128)S(1)} %reshape.168), kind=kLoop, calls=%fused_computation.1 | loop fusion | flops 737280 | bytes 2257920 | tf_op jit(solution)/shard_map/while/body/eval_jaxpr/convert_element_type | solution.py:70
  42.6 4.9 %convert_bitcast_fusion = bf16[32,20,24,24]{1,3,2,0:T(8,128)(2,1)} fusion(bf16[32,20,24,24]{3,2,1,0:T(8,128)(2,1)S(1)} %multiply_convert_fusion.1), kind=kOutput, calls=%fused_computation.4 | convolution fusion | flops 15118640 | bytes 1474560 | tf_op jit(solution)/shard_map/while/body/eval_jaxpr/ax,pxyz->payz/dot_general | solution.py:37
  47.5 8.5 %copy.11 = bf16[32,20,24,24]{2,3,1,0:T(8,128)(2,1)} copy(bf16[32,20,24,24]{1,3,2,0:T(8,128)(2,1)} %convert_bitcast_fusion) | data formatting | bytes 1474560 | tf_op jit(solution)/shard_map/while/body/eval_jaxpr/convert_element_type | solution.py:39
  56.0 5.2 %fusion.42 = bf16[32,20,24,24]{3,2,1,0:T(8,128)(2,1)} fusion(bf16[32,20,24,24]{2,3,1,0:T(8,128)(2,1)} %copy.11), kind=kOutput, calls=%fused_computation.68 | convolution fusion | flops 17701056 | bytes 1474560 | tf_op jit(solution)/shard_map/while/body/eval_jaxpr/by,pxyz->pxbz/dot_general | solution.py:40
  61.5 7.4 %fusion.2 = bf16[32,20,24,24]{3,2,1,0:T(8,128)(2,1)} fusion(f32[20,24,24]{2,1,0:T(8,128)S(1)} %fusion.19, bf16[32,20,24,24]{3,2,1,0:T(8,128)(2,1)} %fusion.42), kind=kOutput, calls=%fused_computation.5 | convolution fusion | flops 36139392 | bytes 1520640 | tf_op jit(solution)/shard_map/while/body/eval_jaxpr/cz,pxyz->pxyc/dot_general | solution.py:45
  68.9 5.4 %convert_bitcast_fusion.1 = bf16[32,20,24,24]{2,3,1,0:T(8,128)(2,1)} fusion(bf16[32,20,24,24]{3,2,1,0:T(8,128)(2,1)} %fusion.2), kind=kOutput, calls=%fused_computation.8 | convolution fusion | flops 18069696 | bytes 1474560 | tf_op jit(solution)/shard_map/while/body/eval_jaxpr/by,pxyz->pxbz/dot_general | solution.py:48
  74.3 10.1 %copy.14 = bf16[32,20,24,24]{0,1,3,2:T(8,128)(2,1)S(1)} copy(bf16[32,20,24,24]{2,3,1,0:T(8,128)(2,1)} %convert_bitcast_fusion.1) | data formatting | bytes 1474560 | tf_op jit(solution)/shard_map/while/body/eval_jaxpr/convert_element_type | solution.py:50
  84.4 4.0 %convolution_bitcast_fusion = f32[32,20,24,24]{0,1,3,2:T(8,128)} fusion(bf16[32,20,24,24]{0,1,3,2:T(8,128)(2,1)S(1)} %copy.14), kind=kOutput, calls=%fused_computation.13 | convolution fusion | flops 14750000 | bytes 2211840 | tf_op jit(solution)/shard_map/while/body/eval_jaxpr/ax,pxyz->payz/dot_general | solution.py:51
  88.4 12.1 %copy.15 = f32[32,20,24,24]{3,2,1,0:T(8,128)} copy(f32[32,20,24,24]{0,1,3,2:T(8,128)} %convolution_bitcast_fusion) | data formatting | bytes 2949120 | tf_op jit(solution)/shard_map/while/body/eval_jaxpr/ax,pxyz->payz/transpose | solution.py:51
  102.0 6.8 %reshape.165 = f32[32,11520]{1,0:T(8,128)S(1)} reshape(f32[32,20,24,24]{3,2,1,0:T(8,128)} %copy.15) | data formatting | bytes 2949120 | tf_op jit(solution)/shard_map/while/body/eval_jaxpr/reshape | solution.py:72
  108.9 29.9 %all-reduce = bf16[32]{0:T(256)(128)(2,1)S(1)} all-reduce(bf16[32]{0:T(256)(128)(2,1)S(1)} %dynamic-update-slice.3), channel_id=1, replica_groups=mesh['orb'=16,'grid'=2] {'orb'}, use_global_device_ids=true, to_apply=%add | all-reduce | flops 32 | bytes 128
  139.1 0.7 sub.25
  139.7 3.3 %all-to-all-start = ((f32[1,2,5760]{2,0,1:T(1,128)}), f32[1,2,5760]{2,0,1:T(1,128)S(1)}, u32[]{:S(2)}, u32[]{:S(2)}) async-start(f32[1,2,5760]{2,0,1:T(1,128)} %sub.25), calls=%async_computation | async-start | bytes 92160 | tf_op jit(solution)/shard_map/all_to_all | solution.py:96
  143.8 3.2 %all-to-all-done = f32[1,2,5760]{2,0,1:T(1,128)S(1)} async-done(((f32[1,2,5760]{2,0,1:T(1,128)}), f32[1,2,5760]{2,0,1:T(1,128)S(1)}, u32[]{:S(2)}, u32[]{:S(2)}) %all-to-all-start) | async-done | bytes 46112 | tf_op jit(solution)/shard_map/all_to_all | solution.py:96
  147.0 3.5 %all-to-all-start.2 = ((f32[2,16,360]{2,0,1:T(2,128)}), f32[2,16,360]{2,0,1:T(2,128)S(1)}, u32[]{:S(2)}, u32[]{:S(2)}) async-start(f32[2,16,360]{2,0,1:T(2,128)} %copy.17), calls=%async_computation.2 | async-start | bytes 98304 | tf_op jit(solution)/shard_map/all_to_all | solution.py:98
  150.8 0.6 copy.16
  151.4 5.8 %all-to-all-done.2 = f32[2,16,360]{2,0,1:T(2,128)S(1)} async-done(((f32[2,16,360]{2,0,1:T(2,128)}), f32[2,16,360]{2,0,1:T(2,128)S(1)}, u32[]{:S(2)}, u32[]{:S(2)}) %all-to-all-start.2) | async-done | bytes 46112 | tf_op jit(solution)/shard_map/all_to_all | solution.py:98
  157.3 3.5 %all-to-all-start.1 = ((f32[2,16,360]{2,0,1:T(2,128)}), f32[2,16,360]{2,0,1:T(2,128)S(1)}, u32[]{:S(2)}, u32[]{:S(2)}) async-start(f32[2,16,360]{2,0,1:T(2,128)} %copy.16), calls=%async_computation.1 | async-start | bytes 98304 | tf_op jit(solution)/shard_map/all_to_all | solution.py:101
  160.8 6.7 %all-to-all-done.1 = f32[2,16,360]{2,0,1:T(2,128)S(1)} async-done(((f32[2,16,360]{2,0,1:T(2,128)}), f32[2,16,360]{2,0,1:T(2,128)S(1)}, u32[]{:S(2)}, u32[]{:S(2)}) %all-to-all-start.1) | async-done | bytes 46112 | tf_op jit(solution)/shard_map/all_to_all | solution.py:101
  167.7 38.0 %psum.7 = f32[32,32]{0,1:T(8,128)S(1)} all-reduce(f32[32,32]{0,1:T(8,128)S(1)} %fusion.17), channel_id=1, replica_groups=mesh['orb'=16,'grid'=2] {'orb','grid'}, use_global_device_ids=true, to_apply=%region_1.2 | all-reduce | flops 1024 | bytes 8192 | tf_op jit(solution)/shard_map/psum | solution.py:112
  205.8 2.9 %cholesky.17 = f32[32,32]{1,0:T(8,128)S(1)} custom-call(f32[32,32]{1,0:T(8,128)S(1)} %fusion.24), custom_call_target="Cholesky" | custom-call | tf_op jit(solution)/shard_map/jit(cholesky)/cholesky | solution.py:113
  208.8 0.6 compare_reduce_fusion
  209.4 0.7 fusion.21
  210.1 2.4 %custom-call.6 = f32[1,32,32]{1,2,0:T(8,128)S(1)} custom-call(f32[1,32,32]{2,1,0:T(8,128)S(1)} %fusion.21), custom_call_target="InvertDiagBlocksLowerTriangular" | custom-call | tf_op jit(solution)/shard_map/triangular_solve | solution.py:115
  222.4 5.0 %all-to-all-start.3 = ((f32[16,2,360]{2,1,0:T(2,128)}), f32[16,2,360]{2,1,0:T(2,128)S(1)}, u32[]{:S(2)}, u32[]{:S(2)}) async-start(f32[16,2,360]{2,1,0:T(2,128)} %constant_dynamic-update-slice_fusion), calls=%async_computation.3 | async-start | bytes 98304 | tf_op jit(solution)/shard_map/all_to_all | solution.py:118
  227.4 0.6 copy.30
  228.0 6.1 %all-to-all-done.3 = f32[16,2,360]{2,1,0:T(2,128)S(1)} async-done(((f32[16,2,360]{2,1,0:T(2,128)}), f32[16,2,360]{2,1,0:T(2,128)S(1)}, u32[]{:S(2)}, u32[]{:S(2)}) %all-to-all-start.3) | async-done | bytes 46112 | tf_op jit(solution)/shard_map/all_to_all | solution.py:118
  234.1 0.8 reshape.167
  (50 shorter events, 12.9 us)
Async XLA Ops:
  88.4 12.1 %copy-start.3 = (u32[32]{0:T(128)S(1)}, u32[32]{0:T(128)}, u32[]{:S(2)}) copy-start(u32[32]{0:T(128)} %constant.125) | copy-start | bytes 388
  88.4 13.4 %copy-start.2 = (bf16[2]{0:T(256)(128)(2,1)S(1)}, bf16[2]{0:T(256)(128)(2,1)}, u32[]{:S(2)}) copy-start(bf16[2]{0:T(256)(128)(2,1)} %param.3) | copy-start | bytes 16
  102.0 36.7 %copy-start = (f32[32,11520]{1,0:T(8,128)S(1)}, f32[32,11520]{1,0:T(8,128)}, u32[]{:S(2)}) copy-start(f32[32,11520]{1,0:T(8,128)} %reshape.176) | copy-start | bytes 4423684
  102.0 41.0 %copy-start.1 = (bf16[2,5760]{1,0:T(2,128)(2,1)S(1)}, bf16[2,5760]{1,0:T(2,128)(2,1)}, u32[]{:S(2)}) copy-start(bf16[2,5760]{1,0:T(2,128)(2,1)} %param.2) | copy-start | bytes 69124
  139.7 7.3 %all-to-all-start = ((f32[1,2,5760]{2,0,1:T(1,128)}), f32[1,2,5760]{2,0,1:T(1,128)S(1)}, u32[]{:S(2)}, u32[]{:S(2)}) async-start(f32[1,2,5760]{2,0,1:T(1,128)} %sub.25), calls=%async_computation | async-start | bytes 92160 | tf_op jit(solution)/shard_map/all_to_all | solution.py:96
  147.0 10.2 %all-to-all-start.2 = ((f32[2,16,360]{2,0,1:T(2,128)}), f32[2,16,360]{2,0,1:T(2,128)S(1)}, u32[]{:S(2)}, u32[]{:S(2)}) async-start(f32[2,16,360]{2,0,1:T(2,128)} %copy.17), calls=%async_computation.2 | async-start | bytes 98304 | tf_op jit(solution)/shard_map/all_to_all | solution.py:98
  157.3 10.2 %all-to-all-start.1 = ((f32[2,16,360]{2,0,1:T(2,128)}), f32[2,16,360]{2,0,1:T(2,128)S(1)}, u32[]{:S(2)}, u32[]{:S(2)}) async-start(f32[2,16,360]{2,0,1:T(2,128)} %copy.16), calls=%async_computation.1 | async-start | bytes 98304 | tf_op jit(solution)/shard_map/all_to_all | solution.py:101
  222.4 11.8 %all-to-all-start.3 = ((f32[16,2,360]{2,1,0:T(2,128)}), f32[16,2,360]{2,1,0:T(2,128)S(1)}, u32[]{:S(2)}, u32[]{:S(2)}) async-start(f32[16,2,360]{2,1,0:T(2,128)} %constant_dynamic-update-slice_fusion), calls=%async_computation.3 | async-start | bytes 98304 | tf_op jit(solution)/shard_map/all_to_all | solution.py:118
